TPU v7x, 32 devices: a whole 2x2x4 slice. The times are simulated.
32 devices in a mesh: dp: 8 (over y, x, core), mp: 4 (over z).
Axes of the slice: x: 2, y: 2, z: 4, core: 2. Of those that a mesh axis runs over, the one named last changes fastest.
Arguments:
- hidden_in: bfloat16 [2, 32, 4096], P(None, 'dp', 'mp'), may hold values from -6 to 6
- rec_gain: float32 [2, 4096], replicated, may hold values from 0.5 to 1.5
- rec_in_x: bfloat16 [2, 4096, 4096], P(None, 'dp', 'mp'), may hold values from -0.09375 to 0.09375
- rec_in_y: bfloat16 [2, 4096, 4096], P(None, 'dp', 'mp'), may hold values from -0.09375 to 0.09375
- conv_weight: float32 [2, 4, 4096], P(None, None, 'mp'), may hold values from -3 to 3
- conv_bias: float32 [2, 4096], P(None, 'mp'), may hold values from -3 to 3
- gate_x_weight: bfloat16 [2, 16, 256, 256], P(None, 'mp'), may hold values from -0.375 to 0.375
- gate_x_bias: float32 [2, 4096], P(None, 'mp'), may hold values from -4 to 4
- gate_a_weight: bfloat16 [2, 16, 256, 256], P(None, 'mp'), may hold values from -0.375 to 0.375
- gate_a_bias: float32 [2, 4096], P(None, 'mp'), may hold values from -4 to 4
- decay_param: float32 [2, 4096], P(None, 'mp'), may hold values from -9 to -1
- rec_out: bfloat16 [2, 4096, 4096], P(None, 'dp', 'mp'), may hold values from -0.09375 to 0.09375
- lru_state: bfloat16 [2, 32, 4096], P(None, 'dp', 'mp'), may hold values from -6 to 6
- conv_state: bfloat16 [2, 3, 32, 4096], P(None, None, 'dp', 'mp'), may hold values from -6 to 6
- scale_index: int32 [2], replicated, may hold values from 0 to 7
- attn_gain: float32 [4096], replicated, may hold values from 0.5 to 1.5
- attn_q: bfloat16 [4096, 4096], P('dp', 'mp'), may hold values from -0.09375 to 0.09375
- attn_kv: bfloat16 [4096, 512], P('dp', 'mp'), may hold values from -0.09375 to 0.09375
- attn_out: bfloat16 [4096, 4096], P('dp', 'mp'), may hold values from -0.09375 to 0.09375
- key_cache: bfloat16 [32, 2048, 256], P('dp', 'mp'), may hold values from -400 to 400
- value_cache: bfloat16 [32, 2048, 256], P('dp', 'mp'), may hold values from -6 to 6
- positions: int32 [32], P('dp'), may hold values from 1 to 6143
Outputs:
- hidden_out: bfloat16 [2, 32, 4096], P(None, 'dp', 'mp')
- lru_out: bfloat16 [2, 32, 4096], P(None, 'dp', 'mp')
- conv_out: bfloat16 [2, 3, 32, 4096], P(None, None, 'dp', 'mp')
- new_kv: bfloat16 [2, 32, 512], P(None, 'dp', 'mp')
Inputs may be any that keep to these rules, and one draw needn't show every extreme that they name: `positions`: the count of tokens a sequence has seen; the cache holds its last min(that count, 2048) tokens.
All inputs are finite; a program needn't handle non-finite values.
Results may differ from a plain program's by a relative error of at most 0.03.
Values may be sent and summed in bfloat16 or wider, within the bound.
A program may use at most 64 MiB of HBM per device.

v0:
```python
import jax
import jax.numpy as jnp
from jax import lax
from jax.sharding import PartitionSpec as P

HEADS = 16
HEAD_DIM = 256
WIN = 2048
LAYERS = 2
STEPS = 2


def joined(array, axis, join):
    gathered = jax.tree.map(
        lambda a, kind: lax.all_gather(a.astype(kind), axis),
        array,
        (jnp.bfloat16, jnp.bfloat16, jnp.bfloat16),
    )

    def take(source):
        return jax.tree.map(
            lambda a, own: lax.dynamic_index_in_dim(a, source, 0, False).astype(own.dtype),
            gathered,
            array,
        )

    return lax.fori_loop(
        1, lax.axis_size(axis), lambda source, state: join(state, take(source)), take(0)
    )


def norm_rows(values, gain):
    mean_sq = jnp.mean(values * values, axis=-1, keepdims=True)
    return (values * lax.rsqrt(mean_sq + 1e-06) * gain).astype(jnp.bfloat16)


def spread_project(normed, weight):
    spread = lax.all_to_all(normed, "dp", split_axis=1, concat_axis=0, tiled=True)
    return lax.psum_scatter(
        jnp.dot(spread, weight, preferred_element_type=jnp.float32),
        "dp",
        scatter_dimension=0,
        tiled=True,
    )


def full_stream(stream):
    return lax.all_gather(stream, "mp", axis=1, tiled=True)


def full_features(values):
    return lax.all_gather(values, "mp", axis=1, tiled=True)


def lru_gate(filtered_half, weight, bias):
    rows = filtered_half.shape[0]
    shaped = filtered_half.reshape(rows, weight.shape[0], weight.shape[1])
    mixed = jnp.einsum("bhi,hij->bhj", shaped, weight, preferred_element_type=jnp.float32)
    return jax.nn.sigmoid(mixed.reshape(rows, -1) + bias)


def combine(first, second):
    top_first, total_first, summed_first = first
    top_second, total_second, summed_second = second
    best = jnp.maximum(top_first, top_second)
    fade_first = jnp.exp(top_first - best)
    fade_second = jnp.exp(top_second - best)
    total = total_first * fade_first + total_second * fade_second
    summed = summed_first * fade_first[..., None] + summed_second * fade_second[..., None]
    return (best, total, summed)


def recurrent_layer(
    stream,
    gain,
    in_x,
    in_y,
    conv_taps,
    conv_shift,
    gx_weight,
    gx_bias,
    ga_weight,
    ga_bias,
    decay,
    out_weight,
    state,
    window,
):
    normed = norm_rows(full_stream(stream), gain)
    width = in_x.shape[1]
    both = spread_project(normed, jnp.concatenate([in_x, in_y], axis=1))
    branch_input = both[:, :width]
    branch_gate = both[:, width:]
    driven = branch_input.astype(jnp.bfloat16)
    gating = jax.nn.gelu(branch_gate, approximate=True)
    taps = jnp.concatenate([window, driven[None]], 0)
    filtered = jnp.sum(taps.astype(jnp.float32) * conv_taps[:, None, :], axis=0) + conv_shift
    filtered_half = filtered.astype(jnp.bfloat16)
    input_gate = lru_gate(filtered_half, gx_weight, gx_bias)
    decay_gate = lru_gate(filtered_half, ga_weight, ga_bias)
    log_decay = -8.0 * decay_gate * jax.nn.softplus(decay)
    state = jnp.exp(log_decay) * state + jnp.sqrt(1.0 - jnp.exp(2.0 * log_decay)) * (
        input_gate * filtered
    )
    mixed = (state * gating).astype(jnp.bfloat16)
    stream = stream + spread_project(full_features(mixed), out_weight)
    return (stream, state, taps[1:])


def attention_layer(
    stream,
    gain,
    w_query,
    w_keyvalue,
    w_out,
    key_cache,
    value_cache,
    positions,
    fresh_keys,
    fresh_values,
    step,
):
    normed = norm_rows(full_stream(stream), gain)
    query_cols = w_query.shape[1]
    local = spread_project(normed, jnp.concatenate([w_query, w_keyvalue], axis=1)).astype(
        jnp.bfloat16
    )
    kv_local = local[:, query_cols:]
    rows = local.shape[0]
    groups = full_features(local).reshape(rows, -1, local.shape[1])
    query = groups[:, :, :query_cols].reshape(rows, HEADS, HEAD_DIM)
    key_value = groups[:, :, query_cols:].reshape(rows, 2 * HEAD_DIM)
    fresh_keys.append(key_value[:, :HEAD_DIM])
    fresh_values.append(key_value[:, HEAD_DIM:])
    slots = key_cache.shape[1]
    slot_ids = lax.axis_index("mp") * slots + jnp.arange(slots, dtype=jnp.int32)
    position = positions[:, None]
    held = position - 1 - jnp.mod(position - 1 - slot_ids[None, :], WIN)
    valid = ((held >= 0) & (held >= position + step - WIN + 1))[:, None, :]
    scores = jnp.einsum(
        "bhd,bsd->bhs", query, key_cache, preferred_element_type=jnp.float32
    ) * HEAD_DIM ** (-0.5)
    masked = jnp.where(valid, scores, -1e30)
    top = jnp.max(masked, axis=-1)
    weights = jnp.where(valid, jnp.exp(masked - top[..., None]), 0.0)
    total = jnp.sum(weights, axis=-1)
    summed = jnp.einsum(
        "bhs,bsd->bhd",
        weights.astype(jnp.bfloat16),
        value_cache,
        preferred_element_type=jnp.float32,
    )
    top, total, summed = joined((top, total, summed), "mp", combine)
    new_keys = jnp.stack(fresh_keys, 1)
    new_values = jnp.stack(fresh_values, 1)
    fresh_scores = jnp.einsum(
        "bhd,bnd->bhn", query, new_keys, preferred_element_type=jnp.float32
    ) * HEAD_DIM ** (-0.5)
    best = jnp.maximum(top, jnp.max(fresh_scores, axis=-1))
    fade = jnp.exp(top - best)
    fresh_weights = jnp.exp(fresh_scores - best[..., None])
    total = total * fade + jnp.sum(fresh_weights, axis=-1)
    summed = summed * fade[..., None] + jnp.einsum(
        "bhn,bnd->bhd",
        fresh_weights.astype(jnp.bfloat16),
        new_values,
        preferred_element_type=jnp.float32,
    )
    attended = (summed / total[..., None]).astype(jnp.bfloat16).reshape(rows, HEADS * HEAD_DIM)
    stream = stream + spread_project(attended, w_out)
    return (stream, kv_local)


def body(
    hidden_in,
    rec_gain,
    rec_in_x,
    rec_in_y,
    conv_weight,
    conv_bias,
    gate_x_weight,
    gate_x_bias,
    gate_a_weight,
    gate_a_bias,
    decay_param,
    rec_out,
    lru_state,
    conv_state,
    scale_index,
    attn_gain,
    attn_q,
    attn_kv,
    attn_out,
    key_cache,
    value_cache,
    positions,
):
    scales = 2.0 ** ((scale_index.astype(jnp.float32) - 4.0) * 0.5)
    states = [lru_state[layer].astype(jnp.float32) * scales[layer] for layer in range(LAYERS)]
    windows = [conv_state[layer] for layer in range(LAYERS)]
    fresh_keys = []
    fresh_values = []
    outputs = []
    kv_parts = []
    for step in range(STEPS):
        stream = hidden_in[step].astype(jnp.float32)
        for layer in range(LAYERS):
            stream, states[layer], windows[layer] = recurrent_layer(
                stream,
                rec_gain[layer],
                rec_in_x[layer],
                rec_in_y[layer],
                conv_weight[layer],
                conv_bias[layer],
                gate_x_weight[layer],
                gate_x_bias[layer],
                gate_a_weight[layer],
                gate_a_bias[layer],
                decay_param[layer],
                rec_out[layer],
                states[layer],
                windows[layer],
            )
        stream, kv_local = attention_layer(
            stream,
            attn_gain,
            attn_q,
            attn_kv,
            attn_out,
            key_cache,
            value_cache,
            positions,
            fresh_keys,
            fresh_values,
            step,
        )
        kv_parts.append(kv_local)
        outputs.append(stream.astype(jnp.bfloat16))
    lru_new = jnp.stack(
        [(states[layer] / scales[layer]).astype(jnp.bfloat16) for layer in range(LAYERS)], 0
    )
    return (jnp.stack(outputs, 0), lru_new, jnp.stack(windows, 0), jnp.stack(kv_parts, 0))


def solution(mesh):
    placed = (
        P(None, "dp", "mp"),
        P(),
        P(None, "dp", "mp"),
        P(None, "dp", "mp"),
        P(None, None, "mp"),
        P(None, "mp"),
        P(None, "mp", None, None),
        P(None, "mp"),
        P(None, "mp", None, None),
        P(None, "mp"),
        P(None, "mp"),
        P(None, "dp", "mp"),
        P(None, "dp", "mp"),
        P(None, None, "dp", "mp"),
        P(),
        P(),
        P("dp", "mp"),
        P("dp", "mp"),
        P("dp", "mp"),
        P("dp", "mp", None),
        P("dp", "mp", None),
        P("dp"),
    )
    return jax.shard_map(
        body,
        mesh=mesh,
        in_specs=placed,
        out_specs=(
            P(None, "dp", "mp"),
            P(None, "dp", "mp"),
            P(None, None, "dp", "mp"),
            P(None, "dp", "mp"),
        ),
        check_vma=False,
    )
```

profile of v0, /device:TPU:0, one launch (start us, length us, event | category | flops | bytes accessed | tf_op | source)
XLA Modules:
  0.0 668.5 jit_solution(16265052284147277069)
XLA Ops:
  8.0 14.9 %all-gather.4 = f32[1,4,4096]{2,1,0:T(4,128)S(1)} all-gather(f32[1,4,1024]{2,1,0:T(4,128)S(1)} %get-tuple-element.445), channel_id=6, replica_groups=mesh['dp'=8,'mp'=4] {'mp'}, dimensions={2}, use_global_device_ids=true | all-gather | bytes 81920 | tf_op jit(solution)/shard_map/all_gather | solution.py:48
  23.1 13.3 %all-gather = f32[1,4,4096]{2,1,0:T(4,128)S(1)} all-gather(f32[1,4,1024]{2,1,0:T(4,128)S(1)} %get-tuple-element.444), channel_id=2, replica_groups=mesh['dp'=8,'mp'=4] {'mp'}, dimensions={2}, use_global_device_ids=true | all-gather | bytes 81920 | tf_op jit(solution)/shard_map/all_gather | solution.py:48
  65.6 52.1 %all-reduce.33.cloned.1.call-done = (f32[32,2048]{1,0:T(8,128)}, f32[32,2048]{1,0:T(8,128)}) async-done(((f32[32,2048]{1,0:T(8,128)}, f32[32,2048]{1,0:T(8,128)}), (f32[32,2048]{1,0:T(8,128)}, f32[32,2048]{1,0:T(8,128)})) %all-reduce.33.cloned.1.call-update) | async-done | bytes 524304
  126.6 13.8 %all_gather.75 = bf16[4,4096]{1,0:T(4,128)(2,1)} all-gather(bf16[4,1024]{1,0:T(4,128)(2,1)S(1)} %fusion.125), channel_id=1, replica_groups=mesh['dp'=8,'mp'=4] {'mp'}, dimensions={1}, use_global_device_ids=true | all-gather | bytes 40960 | tf_op jit(solution)/shard_map/all_gather | solution.py:52
  143.8 13.8 %all_gather.65 = bf16[4,4096]{1,0:T(4,128)(2,1)} all-gather(bf16[4,1024]{1,0:T(4,128)(2,1)S(1)} %get-tuple-element.424), channel_id=1, replica_groups=mesh['dp'=8,'mp'=4] {'mp'}, dimensions={1}, use_global_device_ids=true | all-gather | bytes 40960 | tf_op jit(solution)/shard_map/all_gather | solution.py:52
  169.2 52.6 %all-reduce.31.cloned.1.call-done = (f32[32,1024]{1,0:T(8,128)}, f32[32,1024]{1,0:T(8,128)}) async-done(((f32[32,1024]{1,0:T(8,128)}, f32[32,1024]{1,0:T(8,128)}), (f32[32,1024]{1,0:T(8,128)}, f32[32,1024]{1,0:T(8,128)})) %all-reduce.31.cloned.1.call-update) | async-done | bytes 262160
  222.6 13.2 %all_gather.76 = f32[4,4096]{1,0:T(4,128)S(1)} all-gather(f32[4,1024]{1,0:T(4,128)S(1)} %get-tuple-element.441), channel_id=1, replica_groups=mesh['dp'=8,'mp'=4] {'mp'}, dimensions={1}, use_global_device_ids=true | all-gather | bytes 81920 | tf_op jit(solution)/shard_map/all_gather | solution.py:48
  235.9 13.2 %all_gather.66 = f32[4,4096]{1,0:T(4,128)S(1)} all-gather(f32[4,1024]{1,0:T(4,128)S(1)} %get-tuple-element.440), channel_id=1, replica_groups=mesh['dp'=8,'mp'=4] {'mp'}, dimensions={1}, use_global_device_ids=true | all-gather | bytes 81920 | tf_op jit(solution)/shard_map/all_gather | solution.py:48
  272.2 52.5 %all-reduce.29.cloned.1.call-done = (f32[32,2048]{1,0:T(8,128)}, f32[32,2048]{1,0:T(8,128)}) async-done(((f32[32,2048]{1,0:T(8,128)}, f32[32,2048]{1,0:T(8,128)}), (f32[32,2048]{1,0:T(8,128)}, f32[32,2048]{1,0:T(8,128)})) %all-reduce.29.cloned.1.call-update) | async-done | bytes 524304
  331.6 13.9 %all_gather.77 = bf16[4,4096]{1,0:T(4,128)(2,1)} all-gather(bf16[4,1024]{1,0:T(4,128)(2,1)S(1)} %fusion.124), channel_id=1, replica_groups=mesh['dp'=8,'mp'=4] {'mp'}, dimensions={1}, use_global_device_ids=true | all-gather | bytes 40960 | tf_op jit(solution)/shard_map/all_gather | solution.py:52
  349.5 13.9 %all_gather.67 = bf16[4,4096]{1,0:T(4,128)(2,1)} all-gather(bf16[4,1024]{1,0:T(4,128)(2,1)S(1)} %get-tuple-element.422), channel_id=1, replica_groups=mesh['dp'=8,'mp'=4] {'mp'}, dimensions={1}, use_global_device_ids=true | all-gather | bytes 40960 | tf_op jit(solution)/shard_map/all_gather | solution.py:52
  375.2 52.5 %all-reduce.27.cloned.1.call-done = (f32[32,1024]{1,0:T(8,128)}, f32[32,1024]{1,0:T(8,128)}) async-done(((f32[32,1024]{1,0:T(8,128)}, f32[32,1024]{1,0:T(8,128)}), (f32[32,1024]{1,0:T(8,128)}, f32[32,1024]{1,0:T(8,128)})) %all-reduce.27.cloned.1.call-update) | async-done | bytes 262160
  428.5 13.2 %all_gather.68 = f32[4,4096]{1,0:T(4,128)S(1)} all-gather(f32[4,1024]{1,0:T(4,128)S(1)} %dynamic-slice_add_fusion.4), channel_id=1, replica_groups=mesh['dp'=8,'mp'=4] {'mp'}, dimensions={1}, use_global_device_ids=true | all-gather | bytes 81920 | tf_op jit(solution)/shard_map/all_gather | solution.py:48
  442.7 13.2 %all_gather.78 = f32[4,4096]{1,0:T(4,128)S(1)} all-gather(f32[4,1024]{1,0:T(4,128)S(1)} %dynamic-slice_add_fusion.1), channel_id=1, replica_groups=mesh['dp'=8,'mp'=4] {'mp'}, dimensions={1}, use_global_device_ids=true | all-gather | bytes 81920 | tf_op jit(solution)/shard_map/all_gather | solution.py:48
  473.9 25.9 %all-reduce.34 = (bf16[32,1152]{1,0:T(8,128)(2,1)S(1)}, bf16[32,1152]{1,0:T(8,128)(2,1)S(1)}) all-reduce(f32[32,1152]{1,0:T(8,128)} %fusion.177, f32[32,1152]{1,0:T(8,128)S(1)} %fusion.175), channel_id=20, replica_groups=mesh['dp'=8,'mp'=4] {'dp'}, use_global_device_ids=true, to_apply=%region_24.25.clone | all-reduce | flops 73728 | bytes 442368
  499.8 13.2 %all_gather.69 = bf16[4,4608]{1,0:T(4,128)(2,1)S(1)} all-gather(bf16[4,1152]{1,0:T(4,128)(2,1)S(1)} %dynamic-slice_convert_fusion.1), channel_id=1, replica_groups=mesh['dp'=8,'mp'=4] {'mp'}, dimensions={1}, use_global_device_ids=true | all-gather | bytes 46080 | tf_op jit(solution)/shard_map/all_gather | solution.py:52
  513.1 13.2 %all_gather.79 = bf16[4,4608]{1,0:T(4,128)(2,1)S(1)} all-gather(bf16[4,1152]{1,0:T(4,128)(2,1)S(1)} %dynamic-slice_convert_fusion), channel_id=1, replica_groups=mesh['dp'=8,'mp'=4] {'mp'}, dimensions={1}, use_global_device_ids=true | all-gather | bytes 46080 | tf_op jit(solution)/shard_map/all_gather | solution.py:52
  528.5 13.4 %all-gather.3 = bf16[16,16,256]{2,1,0:T(8,128)(2,1)S(1)} all-gather(bf16[4,16,256]{2,1,0:T(8,128)(2,1)S(1)} %convolution_convert_fusion.1), channel_id=5, replica_groups=mesh['dp'=8,'mp'=4] {'mp'}, dimensions={0}, use_global_device_ids=true | all-gather | bytes 163840 | tf_op jit(solution)/shard_map/all_gather | solution.py:15
  541.9 10.8 %all-gather.9 = bf16[4,4,16]{2,1,0:T(4,128)(2,1)S(1)} all-gather(bf16[1,4,16]{2,1,0:T(4,128)(2,1)S(1)} %bitcast.382), channel_id=4, replica_groups=mesh['dp'=8,'mp'=4] {'mp'}, dimensions={0}, use_global_device_ids=true | all-gather | bytes 640 | tf_op jit(solution)/shard_map/all_gather | solution.py:15
  552.7 7.6 %all-gather.8 = bf16[4,4,16]{2,1,0:T(4,128)(2,1)S(1)} all-gather(bf16[1,4,16]{2,1,0:T(4,128)(2,1)S(1)} %convert_bitcast_fusion.3), channel_id=3, replica_groups=mesh['dp'=8,'mp'=4] {'mp'}, dimensions={0}, use_global_device_ids=true | all-gather | bytes 640 | tf_op jit(solution)/shard_map/all_gather | solution.py:15
  564.8 13.4 %all-gather.7 = bf16[16,16,256]{2,1,0:T(8,128)(2,1)S(1)} all-gather(bf16[4,16,256]{2,1,0:T(8,128)(2,1)S(1)} %convolution_convert_fusion), channel_id=9, replica_groups=mesh['dp'=8,'mp'=4] {'mp'}, dimensions={0}, use_global_device_ids=true | all-gather | bytes 163840 | tf_op jit(solution)/shard_map/all_gather | solution.py:15
  578.2 9.6 %all-gather.11 = bf16[4,4,16]{2,1,0:T(4,128)(2,1)S(1)} all-gather(bf16[1,4,16]{2,1,0:T(4,128)(2,1)S(1)} %bitcast.381), channel_id=8, replica_groups=mesh['dp'=8,'mp'=4] {'mp'}, dimensions={0}, use_global_device_ids=true | all-gather | bytes 640 | tf_op jit(solution)/shard_map/all_gather | solution.py:15
  587.8 7.6 %all-gather.10 = bf16[4,4,16]{2,1,0:T(4,128)(2,1)S(1)} all-gather(bf16[1,4,16]{2,1,0:T(4,128)(2,1)S(1)} %convert_bitcast_fusion.1), channel_id=7, replica_groups=mesh['dp'=8,'mp'=4] {'mp'}, dimensions={0}, use_global_device_ids=true | all-gather | bytes 640 | tf_op jit(solution)/shard_map/all_gather | solution.py:15
  608.5 51.3 %all-reduce.25.cloned.1.call-done = (f32[32,1024]{1,0:T(8,128)}, f32[32,1024]{1,0:T(8,128)}) async-done(((f32[32,1024]{1,0:T(8,128)}, f32[32,1024]{1,0:T(8,128)}), (f32[32,1024]{1,0:T(8,128)}, f32[32,1024]{1,0:T(8,128)})) %all-reduce.25.cloned.1.call-update) | async-done | bytes 262160
  (245 shorter events, 142.1 us)
Async XLA Ops:
  7.2 519.2 %copy-start = (bf16[4,512,256]{2,1,0:T(8,128)(2,1)S(1)}, bf16[4,512,256]{2,1,0:T(8,128)(2,1)}, u32[]{:S(2)}) copy-start(bf16[4,512,256]{2,1,0:T(8,128)(2,1)} %param.45) | copy-start | bytes 3145732
  38.1 14.1 %all-to-all-start = ((bf16[4,8,512]{2,0,1:T(4,128)(2,1)}), bf16[4,8,512]{2,0,1:T(4,128)(2,1)S(1)}, u32[]{:S(2)}, u32[]{:S(2)}) async-start(bf16[4,8,512]{2,0,1:T(4,128)(2,1)} %bitcast.12), calls=%async_computation | async-start | bytes 65536 | tf_op jit(solution)/shard_map/all_to_all | solution.py:38
  44.6 81.1 %copy-start.14 = (f32[1,1024]{1,0:T(1,128)}, f32[1,1024]{1,0:T(1,128)S(1)}, u32[]{:S(2)}) copy-start(f32[1,1024]{1,0:T(1,128)S(1)} %get-tuple-element.453) | copy-start | bytes 12292
  52.2 9.0 %all-to-all-start.6 = ((bf16[4,8,512]{2,0,1:T(4,128)(2,1)}), bf16[4,8,512]{2,0,1:T(4,128)(2,1)S(1)}, u32[]{:S(2)}, u32[]{:S(2)}) async-start(bf16[4,8,512]{2,0,1:T(4,128)(2,1)} %bitcast.72), calls=%async_computation.6 | async-start | bytes 65536 | tf_op jit(solution)/shard_map/all_to_all | solution.py:38
  56.4 61.3 %all-reduce.33.cloned.1.call-start = ((), (), s32[]{:S(2)}) async-start(), calls=%async_computation.16 | async-start | bytes 1048576
  63.6 103.0 %copy-start.1 = (bf16[2,512,1024]{2,1,0:T(8,128)(2,1)S(1)}, bf16[2,512,1024]{2,1,0:T(8,128)(2,1)}, u32[]{:S(2)}) copy-start(bf16[2,512,1024]{2,1,0:T(8,128)(2,1)} %param.37) | copy-start | bytes 6291460
  121.8 100.0 %copy-start.9 = (bf16[2,4,1024]{2,1,0:T(4,128)(2,1)S(1)}, bf16[2,4,1024]{2,1,0:T(4,128)(2,1)}, u32[]{:S(2)}) copy-start(bf16[2,4,1024]{2,1,0:T(4,128)(2,1)} %param.26) | copy-start | bytes 49156
  140.4 17.2 %all-to-all-start.7 = ((bf16[4,8,512]{2,0,1:T(4,128)(2,1)}), bf16[4,8,512]{2,0,1:T(4,128)(2,1)S(1)}, u32[]{:S(2)}, u32[]{:S(2)}) async-start(bf16[4,8,512]{2,0,1:T(4,128)(2,1)} %bitcast.80), calls=%async_computation.7 | async-start | bytes 65536 | tf_op jit(solution)/shard_map/all_to_all | solution.py:38
  157.6 9.0 %all-to-all-start.1 = ((bf16[4,8,512]{2,0,1:T(4,128)(2,1)}), bf16[4,8,512]{2,0,1:T(4,128)(2,1)S(1)}, u32[]{:S(2)}, u32[]{:S(2)}) async-start(bf16[4,8,512]{2,0,1:T(4,128)(2,1)} %bitcast.31), calls=%async_computation.1 | async-start | bytes 65536 | tf_op jit(solution)/shard_map/all_to_all | solution.py:38
  161.8 60.0 %all-reduce.31.cloned.1.call-start = ((), (), s32[]{:S(2)}) async-start(), calls=%async_computation.15 | async-start | bytes 524288
  168.5 98.4 %copy-start.5 = (bf16[512,1024]{1,0:T(8,128)(2,1)S(1)}, bf16[512,1024]{1,0:T(8,128)(2,1)}, u32[]{:S(2)}) copy-start(bf16[512,1024]{1,0:T(8,128)(2,1)} %get-tuple-element.428) | copy-start | bytes 3145732
  250.0 8.1 %all-to-all-start.2 = ((bf16[4,8,512]{2,0,1:T(4,128)(2,1)}), bf16[4,8,512]{2,0,1:T(4,128)(2,1)S(1)}, u32[]{:S(2)}, u32[]{:S(2)}) async-start(bf16[4,8,512]{2,0,1:T(4,128)(2,1)} %bitcast.36), calls=%async_computation.2 | async-start | bytes 65536 | tf_op jit(solution)/shard_map/all_to_all | solution.py:38
  258.1 8.1 %all-to-all-start.8 = ((bf16[4,8,512]{2,0,1:T(4,128)(2,1)}), bf16[4,8,512]{2,0,1:T(4,128)(2,1)S(1)}, u32[]{:S(2)}, u32[]{:S(2)}) async-start(bf16[4,8,512]{2,0,1:T(4,128)(2,1)} %bitcast.82), calls=%async_computation.8 | async-start | bytes 65536 | tf_op jit(solution)/shard_map/all_to_all | solution.py:38
  261.4 63.2 %all-reduce.29.cloned.1.call-start = ((), (), s32[]{:S(2)}) async-start(), calls=%async_computation.14 | async-start | bytes 1048576
  329.1 126.9 %copy-start.25 = (f32[4096]{0:T(1024)S(1)}, f32[4096]{0:T(1024)}, u32[]{:S(2)}) copy-start(f32[4096]{0:T(1024)} %param.41) | copy-start | bytes 49156
  345.4 18.0 %all-to-all-start.9 = ((bf16[4,8,512]{2,0,1:T(4,128)(2,1)}), bf16[4,8,512]{2,0,1:T(4,128)(2,1)S(1)}, u32[]{:S(2)}, u32[]{:S(2)}) async-start(bf16[4,8,512]{2,0,1:T(4,128)(2,1)} %bitcast.90), calls=%async_computation.9 | async-start | bytes 65536 | tf_op jit(solution)/shard_map/all_to_all | solution.py:38
  363.4 9.0 %all-to-all-start.3 = ((bf16[4,8,512]{2,0,1:T(4,128)(2,1)}), bf16[4,8,512]{2,0,1:T(4,128)(2,1)S(1)}, u32[]{:S(2)}, u32[]{:S(2)}) async-start(bf16[4,8,512]{2,0,1:T(4,128)(2,1)} %bitcast.55), calls=%async_computation.3 | async-start | bytes 65536 | tf_op jit(solution)/shard_map/all_to_all | solution.py:38
  367.5 60.3 %all-reduce.27.cloned.1.call-start = ((), (), s32[]{:S(2)}) async-start(), calls=%async_computation.13 | async-start | bytes 524288
  442.7 83.7 %copy-start.23 = (pred[4,512]{1,0:T(4,128)(4,1)S(1)}, pred[4,512]{1,0:T(4,128)(4,1)}, u32[]{:S(2)}) copy-start(pred[4,512]{1,0:T(4,128)(4,1)} %get-tuple-element.463) | copy-start | bytes 6148
  456.7 8.1 %all-to-all-start.4 = ((bf16[4,8,512]{2,0,1:T(4,128)(2,1)}), bf16[4,8,512]{2,0,1:T(4,128)(2,1)S(1)}, u32[]{:S(2)}, u32[]{:S(2)}) async-start(bf16[4,8,512]{2,0,1:T(4,128)(2,1)} %bitcast.58), calls=%async_computation.4 | async-start | bytes 65536 | tf_op jit(solution)/shard_map/all_to_all | solution.py:38
  464.8 8.1 %all-to-all-start.10 = ((bf16[4,8,512]{2,0,1:T(4,128)(2,1)}), bf16[4,8,512]{2,0,1:T(4,128)(2,1)S(1)}, u32[]{:S(2)}, u32[]{:S(2)}) async-start(bf16[4,8,512]{2,0,1:T(4,128)(2,1)} %bitcast.92), calls=%async_computation.10 | async-start | bytes 65536 | tf_op jit(solution)/shard_map/all_to_all | solution.py:38
  561.4 35.4 %all-to-all-start.5 = ((bf16[4,8,512]{2,0,1:T(4,128)(2,1)}), bf16[4,8,512]{2,0,1:T(4,128)(2,1)S(1)}, u32[]{:S(2)}, u32[]{:S(2)}) async-start(bf16[4,8,512]{2,0,1:T(4,128)(2,1)} %copy.95), calls=%async_computation.5 | async-start | bytes 65536 | tf_op jit(solution)/shard_map/all_to_all | solution.py:38
  596.9 9.1 %all-to-all-start.11 = ((bf16[4,8,512]{2,0,1:T(4,128)(2,1)}), bf16[4,8,512]{2,0,1:T(4,128)(2,1)S(1)}, u32[]{:S(2)}, u32[]{:S(2)}) async-start(bf16[4,8,512]{2,0,1:T(4,128)(2,1)} %copy.107), calls=%async_computation.11 | async-start | bytes 65536 | tf_op jit(solution)/shard_map/all_to_all | solution.py:38
  601.1 58.7 %all-reduce.25.cloned.1.call-start = ((), (), s32[]{:S(2)}) async-start(), calls=%async_computation.12 | async-start | bytes 524288
  (23 other events, 882.1 us)
Sparse Core Ops, SparseCore 0:
  63.7 53.8 all-reduce.32
  168.6 53.0 all-reduce.30
  270.8 53.8 all-reduce.28
  374.7 53.0 all-reduce.26
  608.0 51.7 all-reduce.24
where the time goes:
time: 671 us; the launch traced here: 669 us
  waiting for transfers between devices  293 us (44%)
  blocking collectives  251 us (37%)
  starting transfers between devices  43.8 us (7%)
  matrix products  25.1 us (4%)
  other arithmetic  20.7 us (3%)
  local copies, waits for them, and re-layouts  20 us (3%)
  between operations  15.2 us (2%)
    unnamed x10, waiting for transfers between devices  261 us
    all_gather x6, blocking collectives, full_features(): return lax.all_gather(values, 'mp', axis=1, tiled=True)  81.7 us
    all_gather x6, blocking collectives, full_stream(): return lax.all_gather(stream, 'mp', axis=1, tiled=True)  81 us
    all_gather x6, blocking collectives, joined(): lax.all_gather(a.astype(kind), axis)  62.3 us
    all_to_all x12, starting transfers between devices, spread_project(): lax.all_to_all(normed, 'dp', split_axis=1, concat_axis=0, tiled=True)  43.7 us
    all_to_all x12, waiting for transfers between devices, spread_project(): lax.all_to_all(normed, 'dp', split_axis=1, concat_axis=0, tiled=True)  31.4 us
    unnamed x1, blocking collectives  25.9 us
    dot_general x12, matrix products, spread_project(): jnp.dot(spread, weight, preferred_element_type=jnp.float32)  15.4 us
  transfers between devices with their start and end apart: 17, of which 13 were waited for; matrix products, arithmetic and copies ran while one was open for 3% of the time, Pallas kernels for 0%

commit v1 on v0

v1 whole, which is shorter than its diff:
```python
import functools

import jax
import jax.numpy as jnp
from jax import lax
from jax.experimental import pallas as pl
from jax.experimental.pallas import tpu as pltpu
from jax.sharding import PartitionSpec as P

MESH = pl.DeviceIdType.MESH
LANES = 128
F32 = jnp.float32
BF16 = jnp.bfloat16


def softplus(v):
    return jnp.maximum(v, 0.0) + jnp.log1p(jnp.exp(-jnp.abs(v)))


def stack_rows(parts):
    return jnp.concatenate(parts, axis=0)


def kernel(nd, nm, dims, *refs):
    layers, steps, batch, width, depth, kv_cols, slots, head = dims
    rows = steps * batch
    per = nd // nm
    n_in = 22
    (
        hidden_hbm, rec_gain_hbm, in_x_hbm, in_y_hbm, conv_w_hbm, conv_b_hbm,
        gx_w_hbm, gx_b_hbm, ga_w_hbm, ga_b_hbm, decay_hbm, rec_out_hbm,
        lru_hbm, conv_s_hbm, scale_ref, attn_gain_hbm, q_w_hbm, kv_w_hbm,
        out_w_hbm, key_hbm, value_hbm, pos_ref,
    ) = refs[:n_in]
    hidden_out, lru_out, conv_out, kv_out = refs[n_in:n_in + 4]
    (
        hidden, rec_gain, in_x, in_y, conv_w, conv_b, gx_w, gx_b, ga_w, ga_b,
        decay, rec_out, lru, conv_s, attn_gain, q_w, kv_w, out_w, keys, values,
        spread_send, spread_recv, in_part, in_send, in_recv, o_part, o_send, o_recv,
        q_part, q_send, q_recv, head_send, head_recv, sum_send, sum_recv, stat_send,
        stat_recv, load_sem, spread_ss, spread_rs, part_ss, part_rs, head_ss,
        head_rs, self_sem,
    ) = refs[n_in + 4:]
    me_d = lax.axis_index("dp")
    me_m = lax.axis_index("mp")
    total = nd * nm
    me = me_d * nm + me_m

    loads = {}

    def load(name, src, dst, slot):
        copy = pltpu.make_async_copy(src, dst, load_sem.at[slot])
        copy.start()
        loads[name] = copy

    slot = 0
    for name, src, dst in (
        ("hidden", hidden_hbm, hidden), ("rec_gain", rec_gain_hbm, rec_gain),
        ("in_x0", in_x_hbm.at[0], in_x.at[0]), ("in_y0", in_y_hbm.at[0], in_y.at[0]),
        ("conv_w", conv_w_hbm, conv_w), ("conv_b", conv_b_hbm, conv_b),
        ("conv_s", conv_s_hbm, conv_s), ("lru", lru_hbm, lru),
        ("gx_b", gx_b_hbm, gx_b), ("ga_b", ga_b_hbm, ga_b), ("decay", decay_hbm, decay),
        ("gx_w", gx_w_hbm, gx_w), ("ga_w", ga_w_hbm, ga_w),
        ("rec_out0", rec_out_hbm.at[0], rec_out.at[0]),
        ("in_x1", in_x_hbm.at[1], in_x.at[1]), ("in_y1", in_y_hbm.at[1], in_y.at[1]),
        ("rec_out1", rec_out_hbm.at[1], rec_out.at[1]),
        ("attn_gain", attn_gain_hbm, attn_gain), ("q_w", q_w_hbm, q_w),
        ("kv_w", kv_w_hbm, kv_w), ("keys", key_hbm, keys), ("values", value_hbm, values),
        ("out_w", out_w_hbm, out_w),
    ):
        load(name, src, dst, slot)
        slot += 1

    barrier = pltpu.get_barrier_semaphore()

    @pl.loop(1, total)
    def _(k):
        target = lax.rem(me + k, total)
        pl.semaphore_signal(
            barrier, inc=1, device_id=(target // nm, lax.rem(target, nm)), device_id_type=MESH
        )

    pl.semaphore_wait(barrier, total - 1)

    own_slot = lax.rem(me_d, per)
    is_mine = me_d // per == me_m

    def spread(phase, block):
        for j in range(per):
            spread_send[phase, j] = block[:, j * depth:(j + 1) * depth]
        for j in range(per):
            for k in range(nm):
                target_m = lax.rem(me_m + k, nm)
                target_d = me_m * per + j
                source = spread_send.at[phase, j]

                def remote(source=source, target_d=target_d, target_m=target_m):
                    pltpu.make_async_remote_copy(
                        src_ref=source, dst_ref=spread_recv.at[phase, me_d],
                        send_sem=spread_ss.at[phase], recv_sem=spread_rs.at[phase],
                        device_id=(target_d, target_m), device_id_type=MESH,
                    ).start()

                if k == 0:
                    pl.when(target_d != me_d)(remote)
                else:
                    remote()

        @pl.when(is_mine)
        def _():
            pltpu.make_async_copy(
                spread_send.at[phase, own_slot], spread_recv.at[phase, me_d], self_sem.at[phase]
            ).start()

        @pl.when(is_mine)
        def _():
            pltpu.make_async_copy(
                spread_send.at[phase, own_slot], spread_recv.at[phase, me_d], self_sem.at[phase]
            ).wait()
            part = spread_recv.at[phase, pl.ds(0, nd - 1)]
            pltpu.make_async_copy(part, part, spread_rs.at[phase]).wait()

        @pl.when(jnp.logical_not(is_mine))
        def _():
            part = spread_recv.at[phase]
            pltpu.make_async_copy(part, part, spread_rs.at[phase]).wait()

        return spread_recv[phase].reshape(nd * rows, depth)

    def reduce_rows(sem_slot, part, send, recv, at):
        for k in range(1, nd):
            target = lax.rem(me_d + k, nd)
            send[at, k - 1] = part[pl.ds(pl.multiple_of(target * rows, rows), rows), :].astype(BF16)
            pltpu.make_async_remote_copy(
                src_ref=send.at[at, k - 1], dst_ref=recv.at[at, k - 1],
                send_sem=part_ss.at[sem_slot], recv_sem=part_rs.at[sem_slot],
                device_id=(target, me_m), device_id_type=MESH,
            ).start()
        mine = part[pl.ds(pl.multiple_of(me_d * rows, rows), rows), :]
        got = recv.at[at]
        pltpu.make_async_copy(got, got, part_rs.at[sem_slot]).wait()
        for k in range(nd - 1):
            mine = mine + recv[at, k].astype(F32)
        return mine

    def normed(gathered, gain):
        wide = gathered.astype(F32)
        squares = jnp.sum(wide * wide, axis=-1, keepdims=True)
        return (wide * gain).astype(BF16), jnp.broadcast_to(squares, (nd * rows, LANES))

    def mean_scale(squares):
        return lax.rsqrt(squares[:, :1] / float(nd * depth) + 1e-06)

    loads["hidden"].wait()
    stream = stack_rows([hidden[s].astype(F32) for s in range(steps)])

    my_block = pl.multiple_of(me_d * depth, LANES)
    for name in ("rec_gain",):
        loads[name].wait()

    for l in range(layers):
        raw = spread(2 * l, stream.astype(BF16))
        h, squares = normed(raw, rec_gain[l:l + 1, pl.ds(my_block, depth)])
        loads["in_x%d" % l].wait()
        loads["in_y%d" % l].wait()
        in_part[:, :width] = jnp.dot(h, in_x[l], preferred_element_type=F32)
        in_part[:, width:2 * width] = jnp.dot(h, in_y[l], preferred_element_type=F32)
        in_part[:, 2 * width:] = squares
        both = reduce_rows(2 * l, in_part, in_send, in_recv, l)
        scale = mean_scale(both[:, 2 * width:])
        driven = (both[:, :width] * scale).astype(BF16).astype(F32)
        gating = jax.nn.gelu(both[:, width:2 * width] * scale, approximate=True)
        if l == 0:
            for name in (
                "conv_w", "conv_b", "conv_s", "lru", "gx_b", "ga_b", "decay", "gx_w", "ga_w"
            ):
                loads[name].wait()
        taps = [conv_s[l, j].astype(F32) for j in range(conv_s.shape[1])]
        taps += [driven[s * batch:(s + 1) * batch] for s in range(steps)]
        count = conv_w.shape[1]
        filtered = conv_b[l:l + 1, :]
        for j in range(count):
            filtered = filtered + conv_w[l, j:j + 1, :] * stack_rows(taps[j:j + steps])
        for j in range(count - 1):
            conv_out[l, j] = taps[steps + j].astype(BF16)
        half = filtered.astype(BF16)
        blocks, size = gx_w.shape[1], gx_w.shape[2]
        gates = []
        for weight, bias in ((gx_w, gx_b), (ga_w, ga_b)):
            mixed = jnp.concatenate(
                [
                    jnp.dot(
                        half[:, k * size:(k + 1) * size], weight[l, k], preferred_element_type=F32
                    )
                    for k in range(blocks)
                ],
                axis=1,
            )
            gates.append(jax.nn.sigmoid(mixed + bias[l:l + 1, :]))
        log_decay = -8.0 * gates[1] * softplus(decay[l:l + 1, :])
        keep = jnp.exp(log_decay)
        add = jnp.sqrt(1.0 - jnp.exp(2.0 * log_decay)) * (gates[0] * filtered)
        index = jnp.full((1, LANES), scale_ref[l], jnp.int32).astype(F32)[:, :1]
        state_scale = jnp.exp2((index - 4.0) * 0.5)
        state = lru[l].astype(F32) * state_scale
        states = []
        for s in range(steps):
            state = keep[s * batch:(s + 1) * batch] * state + add[s * batch:(s + 1) * batch]
            states.append(state)
        lru_out[l] = (state / state_scale).astype(BF16)
        mixed = (stack_rows(states) * gating).astype(BF16)
        spreaded = spread(2 * l + 1, mixed)
        loads["rec_out%d" % l].wait()
        o_part[l] = jnp.dot(spreaded, rec_out[l], preferred_element_type=F32)
        stream = stream + reduce_rows(2 * l + 1, o_part.at[l], o_send, o_recv, l)

    raw = spread(2 * layers, stream.astype(BF16))
    loads["attn_gain"].wait()
    h, squares = normed(raw, attn_gain[:, pl.ds(my_block, depth)])
    loads["q_w"].wait()
    loads["kv_w"].wait()
    q_part[:, :width] = jnp.dot(h, q_w[...], preferred_element_type=F32)
    q_part[:, width:width + kv_cols] = jnp.dot(h, kv_w[...], preferred_element_type=F32)
    q_part[:, width + kv_cols:] = squares
    both = reduce_rows(2 * layers, q_part, q_send, q_recv, 0)
    scale = mean_scale(both[:, width + kv_cols:])
    local = (both[:, :width + kv_cols] * scale).astype(BF16)
    for s in range(steps):
        kv_out[s] = local[s * batch:(s + 1) * batch, width:]
    head_send[...] = local
    for k in range(1, nm):
        pltpu.make_async_remote_copy(
            src_ref=head_send, dst_ref=head_recv.at[me_m],
            send_sem=head_ss.at[0], recv_sem=head_rs.at[0],
            device_id=(me_d, lax.rem(me_m + k, nm)), device_id_type=MESH,
        ).start()
    head_recv[me_m] = local
    window = slots * nm
    row_ids = lax.broadcasted_iota(jnp.int32, (rows, 1), 0)
    row_seq = lax.rem(row_ids, batch)
    row_step = row_ids // batch
    position = jnp.zeros((rows, 1), jnp.int32)
    for b in range(batch):
        position = jnp.where(row_seq == b, pos_ref[b], position)
    column = lax.broadcasted_iota(jnp.int32, (rows, batch * slots), 1)
    slot_id = me_m * slots + lax.rem(column, slots)
    back = lax.rem(position - 1 - slot_id + window, window)
    held = position - 1 - back
    valid = (
        (held >= 0) & (held >= position + row_step - window + 1) & (column // slots == row_seq)
    )
    new_column = lax.broadcasted_iota(jnp.int32, (rows, rows), 1)
    new_valid = (
        (lax.rem(new_column, batch) == row_seq) & (new_column // batch <= row_step) & (me_m == 0)
    )
    loads["keys"].wait()
    loads["values"].wait()
    got = head_recv.at[pl.ds(0, nm - 1)]
    pltpu.make_async_copy(got, got, head_rs.at[0]).wait()
    group = width // head
    heads = nm * group
    query = jnp.concatenate(
        [
            head_recv[m, :, g * head:(g + 1) * head].astype(F32)
            for m in range(nm)
            for g in range(group)
        ],
        axis=0,
    ).astype(BF16)
    fresh = jnp.concatenate([head_recv[m, :, width:] for m in range(nm)], axis=1)
    factor = head ** (-0.5)
    dims_t = (((1,), (1,)), ((), ()))
    cache_keys = keys[...].reshape(batch * slots, head)
    cache_values = values[...].reshape(batch * slots, head)
    scores = lax.dot_general(query, cache_keys, dims_t, preferred_element_type=F32) * factor
    scores = scores.reshape(heads, rows, batch * slots)
    new_scores = lax.dot_general(query, fresh[:, :head], dims_t, preferred_element_type=F32)
    new_scores = (new_scores * factor).reshape(heads, rows, rows)
    scores = jnp.where(valid[None], scores, -1e30)
    new_scores = jnp.where(new_valid[None], new_scores, -1e30)
    top = jnp.maximum(
        jnp.max(scores, axis=-1, keepdims=True), jnp.max(new_scores, axis=-1, keepdims=True)
    )
    weights = jnp.where(valid[None], jnp.exp(scores - top), 0.0)
    new_weights = jnp.where(new_valid[None], jnp.exp(new_scores - top), 0.0)
    weight_sum = jnp.sum(weights, axis=-1, keepdims=True) + jnp.sum(
        new_weights, axis=-1, keepdims=True
    )
    summed = jnp.dot(
        weights.reshape(heads * rows, batch * slots).astype(BF16), cache_values,
        preferred_element_type=F32,
    ) + jnp.dot(
        new_weights.reshape(heads * rows, rows).astype(BF16), fresh[:, head:],
        preferred_element_type=F32,
    )
    top = top.reshape(heads * rows, 1)
    weight_sum = weight_sum.reshape(heads * rows, 1)
    span = group * rows
    lane = lax.broadcasted_iota(jnp.int32, (heads * rows, LANES), 1)
    stats = jnp.where(lane < LANES // 2, top, weight_sum)
    sum_send[...] = summed.astype(BF16).reshape(nm, span, head)
    stat_send[...] = stats.reshape(nm, span, LANES)
    for k in range(1, nm):
        target = lax.rem(me_m + k, nm)
        pltpu.make_async_remote_copy(
            src_ref=sum_send.at[target], dst_ref=sum_recv.at[k - 1],
            send_sem=head_ss.at[1], recv_sem=head_rs.at[1],
            device_id=(me_d, target), device_id_type=MESH,
        ).start()
        pltpu.make_async_remote_copy(
            src_ref=stat_send.at[target], dst_ref=stat_recv.at[k - 1],
            send_sem=head_ss.at[2], recv_sem=head_rs.at[2],
            device_id=(me_d, target), device_id_type=MESH,
        ).start()
    pltpu.make_async_copy(sum_recv, sum_recv, head_rs.at[1]).wait()
    pltpu.make_async_copy(stat_recv, stat_recv, head_rs.at[2]).wait()
    parts = [(sum_send[me_m], stat_send[me_m])]
    parts += [(sum_recv[k], stat_recv[k]) for k in range(nm - 1)]
    tops = [stat[:, :1] for _, stat in parts]
    best = functools.reduce(jnp.maximum, tops)
    fades = [jnp.exp(t - best) for t in tops]
    whole = sum(f * stat[:, LANES // 2:LANES // 2 + 1] for f, (_, stat) in zip(fades, parts))
    mixed = sum(f * part.astype(F32) for f, (part, _) in zip(fades, parts)) / whole
    attended = jnp.concatenate(
        [mixed[g * rows:(g + 1) * rows] for g in range(group)], axis=1
    ).astype(BF16)
    spreaded = spread(2 * layers + 1, attended)
    loads["out_w"].wait()
    o_part[layers] = jnp.dot(spreaded, out_w[...], preferred_element_type=F32)
    stream = stream + reduce_rows(2 * layers + 1, o_part.at[layers], o_send, o_recv, layers)
    for s in range(steps):
        hidden_out[s] = stream[s * batch:(s + 1) * batch].astype(BF16)

    for phase in range(2 * layers + 2):
        @pl.when(is_mine)
        def _(phase=phase):
            part = spread_recv.at[phase, pl.ds(0, nd - 1)]
            pltpu.make_async_copy(part, part, spread_ss.at[phase]).wait()

        @pl.when(jnp.logical_not(is_mine))
        def _(phase=phase):
            part = spread_recv.at[phase]
            pltpu.make_async_copy(part, part, spread_ss.at[phase]).wait()

    for l in range(layers):
        for sem_slot, ref in ((2 * l, in_send), (2 * l + 1, o_send)):
            pltpu.make_async_copy(ref.at[l], ref.at[l], part_ss.at[sem_slot]).wait()
    pltpu.make_async_copy(q_send.at[0], q_send.at[0], part_ss.at[2 * layers]).wait()
    pltpu.make_async_copy(o_send.at[layers], o_send.at[layers], part_ss.at[2 * layers + 1]).wait()
    got = head_recv.at[pl.ds(0, nm - 1)]
    pltpu.make_async_copy(got, got, head_ss.at[0]).wait()
    pltpu.make_async_copy(sum_recv, sum_recv, head_ss.at[1]).wait()
    pltpu.make_async_copy(stat_recv, stat_recv, head_ss.at[2]).wait()


def body(nd, nm, *args):
    (
        hidden_in, rec_gain, in_x, in_y, conv_w, conv_b, gx_w, gx_b, ga_w, ga_b, decay,
        rec_out, lru, conv_s, scale_index, attn_gain, q_w, kv_w, out_w, keys, values, positions,
    ) = args
    steps, batch, width = hidden_in.shape
    layers, depth = in_x.shape[:2]
    kv_cols = kv_w.shape[1]
    slots, head = keys.shape[1:]
    rows = steps * batch
    per = nd // nm
    group = width // head
    span = group * rows
    dims = (layers, steps, batch, width, depth, kv_cols, slots, head)
    attn_gain = attn_gain.reshape(1, -1)
    args = (
        hidden_in, rec_gain, in_x, in_y, conv_w, conv_b, gx_w, gx_b, ga_w, ga_b, decay,
        rec_out, lru, conv_s, scale_index, attn_gain, q_w, kv_w, out_w, keys, values, positions,
    )
    in_smem = (14, 21)
    in_cols = 2 * width + LANES
    q_cols = width + kv_cols + LANES
    phases = 2 * layers + 2
    held = [
        pltpu.VMEM(a.shape, a.dtype) for i, a in enumerate(args) if i not in in_smem
    ]
    any_spec = pl.BlockSpec(memory_space=pl.ANY)
    smem = pl.BlockSpec(memory_space=pltpu.SMEM)
    vmem = pl.BlockSpec(memory_space=pltpu.VMEM)
    return pl.pallas_call(
        functools.partial(kernel, nd, nm, dims),
        out_shape=(
            jax.ShapeDtypeStruct(hidden_in.shape, BF16),
            jax.ShapeDtypeStruct(lru.shape, BF16),
            jax.ShapeDtypeStruct(conv_s.shape, BF16),
            jax.ShapeDtypeStruct((steps, batch, kv_cols), BF16),
        ),
        in_specs=[smem if i in in_smem else any_spec for i in range(len(args))],
        out_specs=(vmem,) * 4,
        scratch_shapes=held + [
            pltpu.VMEM((phases, per, rows, depth), BF16),
            pltpu.VMEM((phases, nd, rows, depth), BF16),
            pltpu.VMEM((nd * rows, in_cols), F32),
            pltpu.VMEM((layers, nd - 1, rows, in_cols), BF16),
            pltpu.VMEM((layers, nd - 1, rows, in_cols), BF16),
            pltpu.VMEM((layers + 1, nd * rows, width), F32),
            pltpu.VMEM((layers + 1, nd - 1, rows, width), BF16),
            pltpu.VMEM((layers + 1, nd - 1, rows, width), BF16),
            pltpu.VMEM((nd * rows, q_cols), F32),
            pltpu.VMEM((1, nd - 1, rows, q_cols), BF16),
            pltpu.VMEM((1, nd - 1, rows, q_cols), BF16),
            pltpu.VMEM((rows, width + kv_cols), BF16),
            pltpu.VMEM((nm, rows, width + kv_cols), BF16),
            pltpu.VMEM((nm, span, head), BF16),
            pltpu.VMEM((nm - 1, span, head), BF16),
            pltpu.VMEM((nm, span, LANES), F32),
            pltpu.VMEM((nm - 1, span, LANES), F32),
            pltpu.SemaphoreType.DMA((23,)),
            pltpu.SemaphoreType.DMA((phases,)),
            pltpu.SemaphoreType.DMA((phases,)),
            pltpu.SemaphoreType.DMA((phases,)),
            pltpu.SemaphoreType.DMA((phases,)),
            pltpu.SemaphoreType.DMA((3,)),
            pltpu.SemaphoreType.DMA((3,)),
            pltpu.SemaphoreType.DMA((phases,)),
        ],
        compiler_params=pltpu.CompilerParams(
            collective_id=0, has_side_effects=True, vmem_limit_bytes=56 * 1024 * 1024
        ),
    )(*args)


def solution(mesh):
    placed = (
        P(None, "dp", "mp"),
        P(),
        P(None, "dp", "mp"),
        P(None, "dp", "mp"),
        P(None, None, "mp"),
        P(None, "mp"),
        P(None, "mp", None, None),
        P(None, "mp"),
        P(None, "mp", None, None),
        P(None, "mp"),
        P(None, "mp"),
        P(None, "dp", "mp"),
        P(None, "dp", "mp"),
        P(None, None, "dp", "mp"),
        P(),
        P(),
        P("dp", "mp"),
        P("dp", "mp"),
        P("dp", "mp"),
        P("dp", "mp", None),
        P("dp", "mp", None),
        P("dp"),
    )
    return jax.shard_map(
        functools.partial(body, mesh.shape["dp"], mesh.shape["mp"]),
        mesh=mesh,
        in_specs=placed,
        out_specs=(
            P(None, "dp", "mp"),
            P(None, "dp", "mp"),
            P(None, None, "dp", "mp"),
            P(None, "dp", "mp"),
        ),
        check_vma=False,
    )
```

time: 671 us -> 75.4 us (0.11)
  waiting for transfers between devices: 293 us -> 0 us
  blocking collectives: 251 us -> 0 us
  Pallas kernels: 0 us -> 69.1 us
  starting transfers between devices: 43.8 us -> 0 us
  matrix products: 25.1 us -> 0 us
  other arithmetic: 20.7 us -> 0 us
  local copies, waits for them, and re-layouts: 20 us -> 5.36 us
  between operations: 15.2 us -> 0.65 us
    unnamed x10 -> x0, waiting for transfers between devices: 261 us -> none
    all_gather x18 -> x0, blocking collectives: 225 us -> none  [the longest x6 81.7 us: full_features(): return lax.all_gather(values, 'mp', axis=1, tiled=True)]
    pallas_call x0 -> x1, Pallas kernels: none -> 69.1 us  [body(): pl.pallas_call(functools.partial(kernel, nd, nm, dims), out_shape=(jax.Sh...]
    all_to_all x12 -> x0, starting transfers between devices: 43.7 us -> none  [spread_project(): lax.all_to_all(normed, 'dp', split_axis=1, concat_axis=0, tiled=True)]
    all_to_all x12 -> x0, waiting for transfers between devices: 31.4 us -> none  [spread_project(): lax.all_to_all(normed, 'dp', split_axis=1, concat_axis=0, tiled=True)]
    unnamed x1 -> x0, blocking collectives: 25.9 us -> none
    dot_general x27 -> x0, matrix products: 25.1 us -> none  [the longest x12 15.4 us: spread_project(): jnp.dot(spread, weight, preferred_element_type=jnp.float32)]
    convert_element_type x17 -> x0, other arithmetic: 10 us -> none  [the longest x4 4.76 us: recurrent_layer(): mixed = (state * gating).astype(jnp.bfloat16)]
  transfers between devices with their start and end apart: 17 -> 0, of which waited for: 13 -> 0; matrix products, arithmetic and copies ran while one was open for 3% -> 0% of each run, Pallas kernels for 0% -> 0%
where the time goes in v1:
time: 75.4 us; the launch traced here: 75.1 us
  Pallas kernels  69.1 us (92%)
  local copies, waits for them, and re-layouts  5.36 us (7%)
    pallas_call x1, Pallas kernels, body(): pl.pallas_call(functools.partial(kernel, nd, nm, dims), out_shape=(jax.Sh...  69.1 us
    unnamed x4, local copies, waits for them, and re-layouts  5.36 us

profile of v1, /device:TPU:0, one launch (start us, length us, event | category | flops | bytes accessed | tf_op | source)
XLA Modules:
  0.0 75.1 jit_solution(17575807328709515239)
XLA Ops:
  0.6 69.1 %shard_map.237 = (bf16[2,4,1024]{2,1,0:T(4,128)(2,1)}, bf16[2,4,1024]{2,1,0:T(4,128)(2,1)}, bf16[2,3,4,1024]{3,2,1,0:T(4,128)(2,1)}, bf16[2,4,128]{2,1,0:T(4,128)(2,1)}) custom-call(bf16[2,4,1024]{2,1,0:T(4,128)(2,1)} %refs_0_.1, f32[2,4096]{1,0:T(2,128)} %refs_1_.1, bf16[2,512,1024]{2,1,0:T(8,128)(2,1)} %refs_2_.1, bf16[2,512,1024]{2,1,0:T(8,128)(2,1)} %refs_3_.1, ...), custom_call_target="tpu_custom_call" | custom-call | tf_op jit(solution)/shard_map/pallas_call | solution.py:385
  69.7 1.3 %copy.30 = bf16[2,4,1024]{2,1,0:T(4,128)(2,1)} copy(bf16[2,4,1024]{2,1,0:T(4,128)(2,1)} %get-tuple-element.8) | data formatting | bytes 32768
  71.1 1.3 %copy.31 = bf16[2,4,1024]{2,1,0:T(4,128)(2,1)} copy(bf16[2,4,1024]{2,1,0:T(4,128)(2,1)} %get-tuple-element.9) | data formatting | bytes 32768
  72.4 1.4 %copy.32 = bf16[2,3,4,1024]{3,2,1,0:T(4,128)(2,1)} copy(bf16[2,3,4,1024]{3,2,1,0:T(4,128)(2,1)} %get-tuple-element.10) | data formatting | bytes 98304
  73.8 1.3 %copy.33 = bf16[2,4,128]{2,1,0:T(4,128)(2,1)} copy(bf16[2,4,128]{2,1,0:T(4,128)(2,1)} %get-tuple-element.11) | data formatting | bytes 4096

commit v2 on v1

--- a/solution.py
+++ b/solution.py
@@ -353,6 +353,16 @@
     pltpu.make_async_copy(stat_recv, stat_recv, head_ss.at[2]).wait()
 
 
+def put_out(*refs):
+    copies = [
+        pltpu.make_async_copy(refs[i], refs[4 + i], refs[8].at[i]) for i in range(4)
+    ]
+    for copy in copies:
+        copy.start()
+    for copy in copies:
+        copy.wait()
+
+
 def body(nd, nm, *args):
     (
         hidden_in, rec_gain, in_x, in_y, conv_w, conv_b, gx_w, gx_b, ga_w, ga_b, decay,
@@ -382,14 +392,10 @@
     any_spec = pl.BlockSpec(memory_space=pl.ANY)
     smem = pl.BlockSpec(memory_space=pltpu.SMEM)
     vmem = pl.BlockSpec(memory_space=pltpu.VMEM)
-    return pl.pallas_call(
+    shapes = (hidden_in.shape, lru.shape, conv_s.shape, (steps, batch, kv_cols))
+    results = pl.pallas_call(
         functools.partial(kernel, nd, nm, dims),
-        out_shape=(
-            jax.ShapeDtypeStruct(hidden_in.shape, BF16),
-            jax.ShapeDtypeStruct(lru.shape, BF16),
-            jax.ShapeDtypeStruct(conv_s.shape, BF16),
-            jax.ShapeDtypeStruct((steps, batch, kv_cols), BF16),
-        ),
+        out_shape=tuple(pltpu.VMEM(shape, BF16) for shape in shapes),
         in_specs=[smem if i in in_smem else any_spec for i in range(len(args))],
         out_specs=(vmem,) * 4,
         scratch_shapes=held + [
@@ -423,6 +429,14 @@
             collective_id=0, has_side_effects=True, vmem_limit_bytes=56 * 1024 * 1024
         ),
     )(*args)
+    return pl.pallas_call(
+        put_out,
+        out_shape=tuple(jax.ShapeDtypeStruct(shape, BF16) for shape in shapes),
+        in_specs=[vmem] * 4,
+        out_specs=(any_spec,) * 4,
+        scratch_shapes=[pltpu.SemaphoreType.DMA((4,))],
+        compiler_params=pltpu.CompilerParams(vmem_limit_bytes=1024 * 1024),
+    )(*results)
 
 
 def solution(mesh):

time: 75.4 us -> 69.9 us (0.927)
  local copies, waits for them, and re-layouts: 5.36 us -> 0 us
    unnamed x4 -> x0, local copies, waits for them, and re-layouts: 5.36 us -> none
    pallas_call x1 -> x2, Pallas kernels: 69.1 us -> 69.1 us  [the longest x1 68.4 us: body(): pl.pallas_call(functools.partial(kernel, nd, nm, dims), out_shape=tuple((...]
where the time goes in v2:
time: 69.9 us; the launch traced here: 69.8 us
  Pallas kernels  69.1 us (99%)
    pallas_call x1, Pallas kernels, body(): pl.pallas_call(functools.partial(kernel, nd, nm, dims), out_shape=tuple((...  68.4 us

profile of v2, /device:TPU:0, one launch (start us, length us, event | category | flops | bytes accessed | tf_op | source)
XLA Modules:
  0.0 69.8 jit_solution(3742255491937601869)
XLA Ops:
  0.6 68.4 %shard_map.237 = (bf16[2,4,1024]{2,1,0:T(4,128)(2,1)S(1)}, bf16[2,4,1024]{2,1,0:T(4,128)(2,1)S(1)}, bf16[2,3,4,1024]{3,2,1,0:T(4,128)(2,1)S(1)}, bf16[2,4,128]{2,1,0:T(4,128)(2,1)S(1)}) custom-call(bf16[2,4,1024]{2,1,0:T(4,128)(2,1)} %refs_0_.1, f32[2,4096]{1,0:T(2,128)} %refs_1_.1, bf16[2,512,1024]{2,1,0:T(8,128)(2,1)} %refs_2_.1, ...), custom_call_target="tpu_custom_call" | custom-call | tf_op jit(solution)/shard_map/pallas_call | solution.py:396
  69.1 0.7 shard_map.238

commit v3 on v2

--- a/solution.py
+++ b/solution.py
@@ -43,8 +43,25 @@
     ) = refs[n_in + 4:]
     me_d = lax.axis_index("dp")
     me_m = lax.axis_index("mp")
-    total = nd * nm
-    me = me_d * nm + me_m
+    own_slot = lax.rem(me_d, per)
+    is_mine = me_d // per == me_m
+
+    barrier = pltpu.get_barrier_semaphore()
+
+    def greet(target_d, target_m):
+        pl.semaphore_signal(
+            barrier, inc=1, device_id=(target_d, target_m), device_id_type=MESH
+        )
+
+    for k in range(nd):
+        source_d = lax.rem(me_d + k, nd)
+        if k == 0:
+            pl.when(jnp.logical_not(is_mine))(lambda: greet(me_d, me_d // per))
+        else:
+            greet(source_d, me_d // per)
+            greet(source_d, me_m)
+    for k in range(1, nm):
+        greet(me_d, lax.rem(me_m + k, nm))
 
     loads = {}
 
@@ -71,19 +88,13 @@
         load(name, src, dst, slot)
         slot += 1
 
-    barrier = pltpu.get_barrier_semaphore()
-
-    @pl.loop(1, total)
-    def _(k):
-        target = lax.rem(me + k, total)
-        pl.semaphore_signal(
-            barrier, inc=1, device_id=(target // nm, lax.rem(target, nm)), device_id_type=MESH
-        )
-
-    pl.semaphore_wait(barrier, total - 1)
-
-    own_slot = lax.rem(me_d, per)
-    is_mine = me_d // per == me_m
+    @pl.when(is_mine)
+    def _():
+        pl.semaphore_wait(barrier, 2 * nd + nm - 3)
+
+    @pl.when(jnp.logical_not(is_mine))
+    def _():
+        pl.semaphore_wait(barrier, 2 * nd + nm - 2)
 
     def spread(phase, block):
         for j in range(per):
@@ -127,7 +138,7 @@
 
         return spread_recv[phase].reshape(nd * rows, depth)
 
-    def reduce_rows(sem_slot, part, send, recv, at):
+    def send_rows(sem_slot, part, send, recv, at):
         for k in range(1, nd):
             target = lax.rem(me_d + k, nd)
             send[at, k - 1] = part[pl.ds(pl.multiple_of(target * rows, rows), rows), :].astype(BF16)
@@ -136,6 +147,8 @@
                 send_sem=part_ss.at[sem_slot], recv_sem=part_rs.at[sem_slot],
                 device_id=(target, me_m), device_id_type=MESH,
             ).start()
+
+    def reduced(sem_slot, part, recv, at):
         mine = part[pl.ds(pl.multiple_of(me_d * rows, rows), rows), :]
         got = recv.at[at]
         pltpu.make_async_copy(got, got, part_rs.at[sem_slot]).wait()
@@ -162,14 +175,17 @@
         raw = spread(2 * l, stream.astype(BF16))
         h, squares = normed(raw, rec_gain[l:l + 1, pl.ds(my_block, depth)])
         loads["in_x%d" % l].wait()
+        in_part[:, :width] = jnp.dot(h, in_x[l], preferred_element_type=F32)
+        in_part[:, width:] = squares
+        send_rows(2 * l, in_part, in_send, in_recv, l)
         loads["in_y%d" % l].wait()
-        in_part[:, :width] = jnp.dot(h, in_x[l], preferred_element_type=F32)
-        in_part[:, width:2 * width] = jnp.dot(h, in_y[l], preferred_element_type=F32)
-        in_part[:, 2 * width:] = squares
-        both = reduce_rows(2 * l, in_part, in_send, in_recv, l)
-        scale = mean_scale(both[:, 2 * width:])
+        y_slot = layers + 1 + l
+        y_sem = 2 * layers + 2 + l
+        o_part[y_slot] = jnp.dot(h, in_y[l], preferred_element_type=F32)
+        send_rows(y_sem, o_part.at[y_slot], o_send, o_recv, y_slot)
+        both = reduced(2 * l, in_part, in_recv, l)
+        scale = mean_scale(both[:, width:])
         driven = (both[:, :width] * scale).astype(BF16).astype(F32)
-        gating = jax.nn.gelu(both[:, width:2 * width] * scale, approximate=True)
         if l == 0:
             for name in (
                 "conv_w", "conv_b", "conv_s", "lru", "gx_b", "ga_b", "decay", "gx_w", "ga_w"
@@ -208,11 +224,14 @@
             state = keep[s * batch:(s + 1) * batch] * state + add[s * batch:(s + 1) * batch]
             states.append(state)
         lru_out[l] = (state / state_scale).astype(BF16)
+        branch = reduced(y_sem, o_part.at[y_slot], o_recv, y_slot) * scale
+        gating = jax.nn.gelu(branch, approximate=True)
         mixed = (stack_rows(states) * gating).astype(BF16)
         spreaded = spread(2 * l + 1, mixed)
         loads["rec_out%d" % l].wait()
         o_part[l] = jnp.dot(spreaded, rec_out[l], preferred_element_type=F32)
-        stream = stream + reduce_rows(2 * l + 1, o_part.at[l], o_send, o_recv, l)
+        send_rows(2 * l + 1, o_part.at[l], o_send, o_recv, l)
+        stream = stream + reduced(2 * l + 1, o_part.at[l], o_recv, l)
 
     raw = spread(2 * layers, stream.astype(BF16))
     loads["attn_gain"].wait()
@@ -222,7 +241,8 @@
     q_part[:, :width] = jnp.dot(h, q_w[...], preferred_element_type=F32)
     q_part[:, width:width + kv_cols] = jnp.dot(h, kv_w[...], preferred_element_type=F32)
     q_part[:, width + kv_cols:] = squares
-    both = reduce_rows(2 * layers, q_part, q_send, q_recv, 0)
+    send_rows(2 * layers, q_part, q_send, q_recv, 0)
+    both = reduced(2 * layers, q_part, q_recv, 0)
     scale = mean_scale(both[:, width + kv_cols:])
     local = (both[:, :width + kv_cols] * scale).astype(BF16)
     for s in range(steps):
@@ -327,7 +347,8 @@
     spreaded = spread(2 * layers + 1, attended)
     loads["out_w"].wait()
     o_part[layers] = jnp.dot(spreaded, out_w[...], preferred_element_type=F32)
-    stream = stream + reduce_rows(2 * layers + 1, o_part.at[layers], o_send, o_recv, layers)
+    send_rows(2 * layers + 1, o_part.at[layers], o_send, o_recv, layers)
+    stream = stream + reduced(2 * layers + 1, o_part.at[layers], o_recv, layers)
     for s in range(steps):
         hidden_out[s] = stream[s * batch:(s + 1) * batch].astype(BF16)
 
@@ -345,6 +366,8 @@
     for l in range(layers):
         for sem_slot, ref in ((2 * l, in_send), (2 * l + 1, o_send)):
             pltpu.make_async_copy(ref.at[l], ref.at[l], part_ss.at[sem_slot]).wait()
+        got = o_send.at[layers + 1 + l]
+        pltpu.make_async_copy(got, got, part_ss.at[2 * layers + 2 + l]).wait()
     pltpu.make_async_copy(q_send.at[0], q_send.at[0], part_ss.at[2 * layers]).wait()
     pltpu.make_async_copy(o_send.at[layers], o_send.at[layers], part_ss.at[2 * layers + 1]).wait()
     got = head_recv.at[pl.ds(0, nm - 1)]
@@ -383,7 +406,7 @@
         rec_out, lru, conv_s, scale_index, attn_gain, q_w, kv_w, out_w, keys, values, positions,
     )
     in_smem = (14, 21)
-    in_cols = 2 * width + LANES
+    in_cols = width + LANES
     q_cols = width + kv_cols + LANES
     phases = 2 * layers + 2
     held = [
@@ -404,9 +427,9 @@
             pltpu.VMEM((nd * rows, in_cols), F32),
             pltpu.VMEM((layers, nd - 1, rows, in_cols), BF16),
             pltpu.VMEM((layers, nd - 1, rows, in_cols), BF16),
-            pltpu.VMEM((layers + 1, nd * rows, width), F32),
-            pltpu.VMEM((layers + 1, nd - 1, rows, width), BF16),
-            pltpu.VMEM((layers + 1, nd - 1, rows, width), BF16),
+            pltpu.VMEM((2 * layers + 1, nd * rows, width), F32),
+            pltpu.VMEM((2 * layers + 1, nd - 1, rows, width), BF16),
+            pltpu.VMEM((2 * layers + 1, nd - 1, rows, width), BF16),
             pltpu.VMEM((nd * rows, q_cols), F32),
             pltpu.VMEM((1, nd - 1, rows, q_cols), BF16),
             pltpu.VMEM((1, nd - 1, rows, q_cols), BF16),
@@ -419,8 +442,8 @@
             pltpu.SemaphoreType.DMA((23,)),
             pltpu.SemaphoreType.DMA((phases,)),
             pltpu.SemaphoreType.DMA((phases,)),
-            pltpu.SemaphoreType.DMA((phases,)),
-            pltpu.SemaphoreType.DMA((phases,)),
+            pltpu.SemaphoreType.DMA((phases + layers,)),
+            pltpu.SemaphoreType.DMA((phases + layers,)),
             pltpu.SemaphoreType.DMA((3,)),
             pltpu.SemaphoreType.DMA((3,)),
             pltpu.SemaphoreType.DMA((phases,)),

time: 69.9 us -> 69 us (0.987)
  Pallas kernels: 69.1 us -> 68.2 us
    pallas_call x1, Pallas kernels: 68.4 us -> 67.5 us  [body(): pl.pallas_call(functools.partial(kernel, nd, nm, dims), out_shape=tuple((...]
where the time goes in v3:
time: 69 us; the launch traced here: 68.8 us
  Pallas kernels  68.2 us (99%)
    pallas_call x1, Pallas kernels, body(): pl.pallas_call(functools.partial(kernel, nd, nm, dims), out_shape=tuple((...  67.5 us

profile of v3, /device:TPU:0, one launch (start us, length us, event | category | flops | bytes accessed | tf_op | source)
XLA Modules:
  0.0 68.8 jit_solution(9738325544668609047)
XLA Ops:
  0.6 67.5 %shard_map.237 = (bf16[2,4,1024]{2,1,0:T(4,128)(2,1)S(1)}, bf16[2,4,1024]{2,1,0:T(4,128)(2,1)S(1)}, bf16[2,3,4,1024]{3,2,1,0:T(4,128)(2,1)S(1)}, bf16[2,4,128]{2,1,0:T(4,128)(2,1)S(1)}) custom-call(bf16[2,4,1024]{2,1,0:T(4,128)(2,1)} %refs_0_.1, f32[2,4096]{1,0:T(2,128)} %refs_1_.1, bf16[2,512,1024]{2,1,0:T(8,128)(2,1)} %refs_2_.1, ...), custom_call_target="tpu_custom_call" | custom-call | tf_op jit(solution)/shard_map/pallas_call | solution.py:419
  68.2 0.7 shard_map.238
